TPU v7x, 32 devices: a whole 2x2x4 slice. The times are simulated.
32 devices in a mesh: field: 2 (over x), ep: 16 (over z, y, core).
Axes of the slice: x: 2, y: 2, z: 4, core: 2. Of those that a mesh axis runs over, the one named last changes fastest.
Arguments:
- images: float32 [64, 16, 256], P(('field', 'ep')), parts along dimension 0, may hold values from -6 to 6
- reference_image: float32 [32, 256], P('field'), parts along dimension 0, may hold values from -6 to 6
- kernels: float32 [16, 23, 23], replicated, may hold values from -0.25 to 0.25
- kernel_index: int32 [64], P(('field', 'ep')), parts along dimension 0, may hold values from 0 to 15
- tile_mask: int32 [64, 16, 2], P(('field', 'ep')), parts along dimension 0, may hold values 0 or 1
- systematics: float32 [64, 40], P('field'), parts along dimension 0, may hold values from -6 to 6
- onsets: int32 [16], P('field'), parts along dimension 0, may hold values from 0 to 27
Outputs:
- coefficients: float32 [48, 32, 256], P(None, ('field', 'ep')), parts along dimension 1
- epoch_scatter: float32 [64], P('field'), parts along dimension 0
There are 2 independent parts, one for each index of `field`. A program takes and returns all parts, laid end to end along the dimension named above; an argument that names none is the same for every part. Nothing has to cross between parts.
All inputs are finite; a program needn't handle non-finite values. No bound on the sum of `tile_mask` on one device may be relied on, other than what follows from the above.
Results may differ from a plain program's by a relative error of at most 0.00011.
Values sent between devices are 32-bit elements; how exact they have to be, the bound alone decides.
A program may use at most 64 MiB of HBM per device.

v0:
```python
import math

import jax
import jax.numpy as jnp
from jax import lax
from jax.sharding import PartitionSpec as P

cov_ridge = 0.5
fit_ridge = 1.0


def correlate(stack, chosen):
    count, rows, width = stack.shape
    side = chosen.shape[1]
    half = (side - 1) // 2
    padded = jnp.pad(stack, ((0, 0), (half, half), (half, half)))
    filters = jnp.transpose(chosen, (1, 2, 0))[:, :, None, :]
    strip = math.gcd(rows, 16)

    def one_strip(start):
        piece = lax.dynamic_slice_in_dim(padded, start, strip + 2 * half, 1)
        result = lax.conv_general_dilated(
            piece[None],
            filters,
            (1, 1),
            "VALID",
            dimension_numbers=("NCHW", "HWIO", "NCHW"),
            feature_group_count=count,
            precision=lax.Precision.HIGHEST,
        )
        return result[0]

    starts = jnp.arange(rows // strip, dtype=jnp.int32) * strip
    strips = lax.map(one_strip, starts)
    return jnp.transpose(strips, (1, 0, 2, 3)).reshape(count, rows, width)


def subtract(stack, reference_image, chosen, masks):
    result = reference_image[None] - correlate(stack, chosen)
    shape = result.shape
    tiles = result.reshape(shape[0], shape[1], shape[2] // 128, 128) * masks[..., None].astype(
        jnp.float32
    )
    return tiles.reshape(shape)


def build_design(systematics, onsets):
    count = systematics.shape[0]
    templates = onsets.shape[0]
    epoch_axis = jnp.arange(count, dtype=jnp.float32)[:, None]
    delays = epoch_axis - onsets[None, :].astype(jnp.float32)
    timescale = (jnp.arange(templates, dtype=jnp.float32) + 1.0) * count / (2.0 * templates)
    transient = jnp.where(
        delays >= 0.0, jnp.exp(-jnp.maximum(delays, 0.0) / timescale[None, :]), 0.0
    )
    return jnp.concatenate([systematics, transient], axis=1)


def fit_matrix(scatter, npixels, design):
    count = design.shape[0]
    columns = design.shape[1]
    covariance = scatter / npixels + cov_ridge * jnp.eye(count, dtype=scatter.dtype)
    lower = jnp.linalg.cholesky(covariance)
    weighted = jax.scipy.linalg.cho_solve((lower, True), design)
    normal = jnp.dot(design.T, weighted, precision=lax.Precision.HIGHEST) + fit_ridge * jnp.eye(
        columns, dtype=scatter.dtype
    )
    lower_fit = jnp.linalg.cholesky(normal)
    return jax.scipy.linalg.cho_solve((lower_fit, True), weighted.T)


def shards(images, reference_image, kernels, kernel_index, tile_mask, systematics, onsets):
    local_count, rows, width = images.shape
    basis = kernels.shape[0]
    side = kernels.shape[1]
    onehot = (kernel_index[:, None] == jnp.arange(basis, dtype=jnp.int32)[None, :]).astype(
        jnp.float32
    )
    chosen = jnp.dot(
        onehot, kernels.reshape(basis, side * side), precision=lax.Precision.HIGHEST
    ).reshape(local_count, side, side)
    difference = subtract(images, reference_image, chosen, tile_mask)
    received = lax.all_to_all(difference, "ep", split_axis=1, concat_axis=0, tiled=True)
    count = received.shape[0]
    block_rows = received.shape[1]
    pixel_data = received.reshape(count, block_rows * width)
    partial_value = jnp.dot(pixel_data, pixel_data.T, precision=lax.Precision.HIGHEST)
    scatter = lax.psum(partial_value, "ep")
    npixels = float(rows * width)
    design = build_design(systematics, onsets)
    fit = fit_matrix(scatter, npixels, design)
    coefficients = jnp.dot(fit, pixel_data, precision=lax.Precision.HIGHEST)
    projector = jnp.eye(count, dtype=jnp.float32) - jnp.dot(
        design, fit, precision=lax.Precision.HIGHEST
    )
    product = jnp.dot(projector, scatter, precision=lax.Precision.HIGHEST)
    epoch_scatter = jnp.sum(product * projector, axis=1) / npixels
    return (coefficients.reshape(design.shape[1], block_rows, width), epoch_scatter)


def solution(mesh):
    in_specs = (
        P(("field", "ep"), None, None),
        P("field", None),
        P(),
        P(("field", "ep")),
        P(("field", "ep"), None, None),
        P("field", None),
        P("field"),
    )
    out_specs = (P(None, ("field", "ep"), None), P("field"))
    return jax.shard_map(shards, mesh=mesh, in_specs=in_specs, out_specs=out_specs, check_vma=False)
```

profile of v0, /device:TPU:0, one launch (start us, length us, event | category | flops | bytes accessed | tf_op | source)
XLA Modules:
  0.0 186.9 jit_solution(5411633704186777744)
XLA Ops:
  0.6 0.8 pad_bitcast_fusion
  1.5 7.8 %copy.30 = f32[1,2,38,278]{1,0,3,2:T(1,128)} copy(f32[1,2,38,278]{3,2,1,0:T(8,128)S(1)} %pad_bitcast_fusion) | data formatting | bytes 169024 | tf_op jit(solution)/shard_map/while/body/eval_jaxpr/broadcast_in_dim | solution.py:23
  9.3 0.1 reshape.61
  9.5 0.1 dot_general.25
  9.6 0.2 convolution_bitcast_fusion.1
  9.8 0.3 copy.31
  10.1 0.7 copy.32
  10.8 82.8 %fusion.21 = f32[1,2,16,256]{1,0,3,2:T(1,128)S(1)} fusion(f32[1,2,38,278]{1,0,3,2:T(1,128)} %copy.30, f32[23,23,1,2]{3,2,1,0:T(1,128)S(1)} %copy.31), kind=kOutput, calls=%fused_computation.46 | convolution fusion | flops 52002816 | bytes 121512 | tf_op jit(solution)/shard_map/while/body/eval_jaxpr/conv_general_dilated | solution.py:22
  93.6 0.9 bitcast_multiply_fusion
  94.5 1.2 copy.33
  95.8 7.4 %all-to-all-start = ((f32[2,16,256]{2,0,1:T(2,128)}), f32[2,16,256]{2,0,1:T(2,128)S(1)}, u32[]{:S(2)}, u32[]{:S(2)}) async-start(f32[2,16,256]{2,0,1:T(2,128)} %copy.33), calls=%async_computation | async-start | bytes 65536 | tf_op jit(solution)/shard_map/all_to_all | solution.py:83
  103.2 6.6 %all-to-all-done = f32[2,16,256]{2,0,1:T(2,128)S(1)} async-done(((f32[2,16,256]{2,0,1:T(2,128)}), f32[2,16,256]{2,0,1:T(2,128)S(1)}, u32[]{:S(2)}, u32[]{:S(2)}) %all-to-all-start) | async-done | bytes 32800 | tf_op jit(solution)/shard_map/all_to_all | solution.py:83
  109.8 0.2 fusion.22
  110.0 57.7 %psum.7 = f32[32,32]{1,0:T(8,128)S(1)} all-reduce(f32[32,32]{1,0:T(8,128)S(1)} %fusion.22), channel_id=1, replica_groups=mesh['field'=2,'ep'=16] {'ep'}, use_global_device_ids=true, to_apply=%region_0.1 | all-reduce | flops 1024 | bytes 8192 | tf_op jit(solution)/shard_map/psum | solution.py:88
  167.8 2.9 %cholesky.34 = f32[32,32]{1,0:T(8,128)S(1)} custom-call(f32[32,32]{1,0:T(8,128)S(1)} %fusion.14), custom_call_target="Cholesky" | custom-call | tf_op jit(solution)/shard_map/jit(cholesky)/cholesky | solution.py:63
  170.7 0.6 compare_reduce_fusion.1
  171.4 0.7 fusion.9
  172.0 2.4 %custom-call.20 = f32[1,32,32]{1,2,0:T(8,128)S(1)} custom-call(f32[1,32,32]{2,1,0:T(8,128)S(1)} %fusion.9), custom_call_target="InvertDiagBlocksLowerTriangular" | custom-call | tf_op jit(solution)/shard_map/jit(_cho_solve)/triangular_solve | solution.py:64
  174.4 0.3 fusion.12
  174.7 0.1 fusion.10
  174.8 0.3 fusion.20
  175.3 4.4 %cholesky.64 = f32[48,48]{1,0:T(8,128)S(1)} custom-call(f32[48,48]{1,0:T(8,128)S(1)} %fusion.8), custom_call_target="Cholesky" | custom-call | tf_op jit(solution)/shard_map/jit(cholesky)/cholesky | solution.py:68
  179.7 0.6 compare_reduce_fusion
  180.3 0.7 fusion.2
  181.0 3.7 %custom-call.21 = f32[1,48,48]{1,2,0:T(8,128)S(1)} custom-call(f32[1,48,48]{2,1,0:T(8,128)S(1)} %fusion.2), custom_call_target="InvertDiagBlocksLowerTriangular" | custom-call | tf_op jit(solution)/shard_map/jit(_cho_solve)/triangular_solve | solution.py:69
  184.7 0.2 fusion.5
  184.8 0.2 fusion.3
  185.0 0.2 convolution_subtract_fusion
  185.2 0.2 convolution_bitcast_fusion
  185.5 0.2 fusion
  185.7 0.5 broadcast_multiply_fusion
  186.2 0.7 copy.38
  (27 shorter events, 0.4 us)
Async XLA Ops:
  1.5 7.8 %copy-start = (f32[16,23,23]{2,0,1:T(8,128)S(1)}, f32[16,23,23]{2,0,1:T(8,128)}, u32[]{:S(2)}) copy-start(f32[16,23,23]{2,0,1:T(8,128)} %param.9) | copy-start | bytes 101572
  1.5 8.1 %copy-start.5 = (s32[2]{0:T(128)S(1)}, s32[2]{0:T(128)}, u32[]{:S(2)}) copy-start(s32[2]{0:T(128)} %param.10) | copy-start | bytes 28
  1.5 8.6 %copy-start.4 = (s32[2,16,2]{1,2,0:T(2,128)S(1)}, s32[2,16,2]{1,2,0:T(2,128)}, u32[]{:S(2)}) copy-start(s32[2,16,2]{1,2,0:T(2,128)} %param.11) | copy-start | bytes 772
  10.8 82.8 %copy-start.2 = (f32[2,16,2]{0,2,1:T(2,128)S(1)}, f32[2,16,2]{0,2,1:T(2,128)}, u32[]{:S(2)}) copy-start(f32[2,16,2]{0,2,1:T(2,128)} %copy.32) | copy-start | bytes 772
  10.8 82.8 %copy-start.3 = (f32[16,256]{1,0:T(8,128)S(1)}, f32[16,256]{1,0:T(8,128)}, u32[]{:S(2)}) copy-start(f32[16,256]{1,0:T(8,128)} %param.8) | copy-start | bytes 49156
  94.5 8.7 %copy-start.6 = (s32[8]{0:T(128)S(1)}, s32[8]{0:T(128)}, u32[]{:S(2)}) copy-start(s32[8]{0:T(128)} %param.13) | copy-start | bytes 100
  94.5 79.9 %copy-start.1 = (f32[32,40]{1,0:T(8,128)S(1)}, f32[32,40]{1,0:T(8,128)}, u32[]{:S(2)}) copy-start(f32[32,40]{1,0:T(8,128)} %param.12) | copy-start | bytes 15364
  95.8 14.1 %all-to-all-start = ((f32[2,16,256]{2,0,1:T(2,128)}), f32[2,16,256]{2,0,1:T(2,128)S(1)}, u32[]{:S(2)}, u32[]{:S(2)}) async-start(f32[2,16,256]{2,0,1:T(2,128)} %copy.33), calls=%async_computation | async-start | bytes 65536 | tf_op jit(solution)/shard_map/all_to_all | solution.py:83
where the time goes:
time: 187 us
  matrix products  84.9 us (45%)
  blocking collectives  57.7 us (31%)
  other arithmetic  17.5 us (9%)
  local copies, waits for them, and re-layouts  12 us (6%)
  starting transfers between devices  7.41 us (4%)
  waiting for transfers between devices  6.57 us (4%)
    conv_general_dilated x1, matrix products, one_strip(): lax.conv_general_dilated(piece[None], filters, (1, 1), 'VALID', dimension...  82.8 us
    psum x1, blocking collectives, shards(): scatter = lax.psum(partial_value, 'ep')  57.7 us
    broadcast_in_dim x2, local copies, waits for them, and re-layouts, one_strip(): piece[None]  8.6 us
    all_to_all x1, starting transfers between devices, shards(): lax.all_to_all(difference, 'ep', split_axis=1, concat_axis=0, tiled=True)  7.41 us
    all_to_all x1, waiting for transfers between devices, shards(): lax.all_to_all(difference, 'ep', split_axis=1, concat_axis=0, tiled=True)  6.57 us
    another operation x3, other arithmetic, fit_matrix(): lower_fit = jnp.linalg.cholesky(normal)  5.05 us
    another operation x2, other arithmetic, fit_matrix(): return jax.scipy.linalg.cho_solve((lower_fit, True), weighted.T)  4.32 us
  transfers between devices with their start and end apart: 1, of which 1 were waited for; matrix products, arithmetic and copies ran while one was open for 0% of the time, Pallas kernels for 0%

commit v1 on v0

v1 whole, which is shorter than its diff:
```python
import functools

import jax
import jax.numpy as jnp
from jax import lax
from jax.experimental import pallas as pl
from jax.experimental.pallas import tpu as pltpu
from jax.sharding import PartitionSpec as P

cov_ridge = 0.5
fit_ridge = 1.0
LANES = 128
HIGHEST = lax.Precision.HIGHEST


def dot(a, b, contract):
    return lax.dot_general(
        a, b, ((contract[0], contract[1]), ((), ())), precision=HIGHEST, preferred_element_type=jnp.float32
    )


def iota(shape, axis):
    return lax.broadcasted_iota(jnp.int32, shape, axis)


def kernel(
    n,
    images_ref,
    reference_ref,
    kernels_ref,
    index_ref,
    mask_ref,
    systematics_ref,
    onsets_ref,
    coefficients_ref,
    epoch_ref,
    table,
    table_t,
    taps,
    shifted,
    send,
    recv,
    pixels,
    part,
    parts,
    work,
    send_sem,
    recv_sem,
    part_send_sem,
    part_recv_sem,
):
    local, rows, width = images_ref.shape
    side = kernels_ref.shape[0]
    half = (side - 1) // 2
    tiles = width // LANES
    block = rows // n
    epochs = local * n
    nsys = systematics_ref.shape[1]
    ntr = onsets_ref.shape[0]
    columns = nsys + ntr
    npixels = float(rows * width)
    pack = max(LANES // epochs, 1)
    me = lax.axis_index("ep")

    barrier = pltpu.get_barrier_semaphore()
    for d in range(1, n):
        pl.semaphore_signal(
            barrier,
            inc=1,
            device_id={"ep": lax.rem(me + d, n)},
            device_id_type=pl.DeviceIdType.MESH,
        )

    depth = side * rows
    padded_depth = taps.shape[1]
    lane = iota((rows, LANES), 1)
    column = iota((rows, width), 1)
    for e in range(local):
        table[...] = jnp.zeros_like(table)
        for a in range(side):
            table[a : a + 1, 0:side] = kernels_ref[a, pl.ds(index_ref[e], 1), :]
        table[side + 1 : side + 1 + tiles, 0:rows] = mask_ref[e].astype(jnp.float32)
        table_t[...] = table[...].T
        kept = jnp.where(iota((side, LANES), 1) < side, table_t[0:side, :], 0.0)
        kept = pltpu.roll(kept, LANES - half, axis=1)
        groups = [jnp.zeros((rows, LANES), jnp.float32) for _ in range(padded_depth // LANES)]
        for b in range(side):
            start = b * rows
            at = start % LANES
            row = jnp.broadcast_to(kept[b : b + 1, :], (rows, LANES))
            turned = pltpu.roll(row, at, axis=1, stride=1, stride_axis=0)
            inside = (lane >= at) & (lane < at + rows)
            groups[start // LANES] = jnp.where(inside, turned, groups[start // LANES])
        for g, value in enumerate(groups):
            taps[:, g * LANES : (g + 1) * LANES] = value
        image = images_ref[e]
        for b in range(side):
            move = b - half
            moved = pltpu.roll(image, (-move) % width, axis=1) if move else image
            inside = (column + move >= 0) & (column + move < width)
            shifted[b * rows : (b + 1) * rows, :] = jnp.where(inside, moved, 0.0)
        if padded_depth > depth:
            shifted[depth:, :] = jnp.zeros((padded_depth - depth, width), jnp.float32)
        difference = reference_ref[...] - dot(taps[...], shifted[...], ((1,), (0,)))
        for t in range(tiles):
            good = table_t[0:rows, side + 1 + t : side + 2 + t]
            piece = difference[:, t * LANES : (t + 1) * LANES] * good
            for r in range(rows):
                slot = (r % block) * tiles * local + t * local + e
                send[r // block, slot : slot + 1, :] = piece[r : r + 1, :]

    pl.semaphore_wait(barrier, n - 1)

    def exchange(source, target, send_sems, recv_sems, d):
        return pltpu.make_async_remote_copy(
            src_ref=source,
            dst_ref=target,
            send_sem=send_sems.at[d],
            recv_sem=recv_sems.at[d],
            device_id={"ep": lax.rem(me + d, n)},
            device_id_type=pl.DeviceIdType.MESH,
        )

    for d in range(1, n):
        exchange(send.at[lax.rem(me + d, n)], recv.at[me], send_sem, recv_sem, d).start()
    recv[me] = send[me]

    work[...] = jnp.zeros_like(work)
    epoch = iota((epochs, LANES), 0).astype(jnp.float32)
    template = iota((epochs, LANES), 1)
    onset = jnp.zeros((epochs, LANES), jnp.float32)
    for k in range(ntr):
        onset = jnp.where(template == k, onsets_ref[k].astype(jnp.float32), onset)
    delays = epoch - onset
    timescale = (template.astype(jnp.float32) + 1.0) * epochs / (2.0 * ntr)
    transient = jnp.where(delays >= 0.0, jnp.exp(-jnp.maximum(delays, 0.0) / timescale), 0.0)
    work[:, epochs : epochs + nsys] = systematics_ref[...]
    work[:, epochs + nsys : epochs + columns] = transient[:, 0:ntr]
    design = work[...]
    outer = dot(design, design, ((1,), (1,)))

    for d in range(1, n):
        source = lax.rem(me - d + n, n)
        exchange(send.at[source], recv.at[source], send_sem, recv_sem, d).wait_recv()
    for j in range(n):
        for q in range(block * tiles):
            pixels[j * local : (j + 1) * local, q * LANES : (q + 1) * LANES] = recv[
                j, q * local : (q + 1) * local, :
            ]
    data = pixels[...]

    partial_scatter = dot(data, data, ((1,), (1,)))
    share = epochs // pack
    if pack > 1:
        work[:, 0:epochs] = partial_scatter
        wide = jnp.where(iota((epochs, work.shape[1]), 1) < epochs, work[...], 0.0)[:, 0:LANES]
        packed = wide[0:share, :]
        for j in range(1, pack):
            packed = packed + pltpu.roll(wide[j * share : (j + 1) * share, :], j * epochs, axis=1)
        part[...] = packed
    else:
        part[...] = partial_scatter
    for d in range(1, n):
        exchange(part, parts.at[me], part_send_sem, part_recv_sem, d).start()
    parts[me] = part[...]
    for d in range(1, n):
        source = lax.rem(me - d + n, n)
        exchange(part, parts.at[source], part_send_sem, part_recv_sem, d).wait_recv()
    total = parts[0]
    for j in range(1, n):
        total = total + parts[j]
    if pack > 1:
        pieces = [total] + [
            pltpu.roll(total, LANES - j * epochs, axis=1) for j in range(1, pack)
        ]
        scatter = jnp.concatenate(pieces, axis=0)[:, 0:epochs]
    else:
        scatter = total

    diagonal = iota((epochs, epochs), 0) == iota((epochs, epochs), 1)
    covariance = scatter * (1.0 / npixels) + jnp.where(diagonal, cov_ridge, 0.0)
    work[:, 0:epochs] = covariance + fit_ridge * outer
    work[:, epochs + columns : 2 * epochs + columns] = covariance
    system = work[...]
    index = iota(system.shape, 0)
    for k in range(epochs):
        pivot_row = system[k : k + 1, :]
        factor = system[:, k : k + 1]
        scaled = pivot_row * (1.0 / system[k : k + 1, k : k + 1])
        system = jnp.where(index == k, scaled, system - factor * scaled)

    fitted = dot(system, data, ((0,), (0,)))
    coefficients_ref[...] = fitted[epochs : epochs + columns, :]
    product = dot(scatter, system, ((1,), (0,))) * system
    work[0:1, :] = jnp.sum(product, axis=0, keepdims=True) * (1.0 / npixels)
    epoch_ref[...] = work[0:1, epochs + columns : 2 * epochs + columns]

    for d in range(1, n):
        exchange(send.at[lax.rem(me + d, n)], recv.at[me], send_sem, recv_sem, d).wait_send()
        exchange(part, parts.at[me], part_send_sem, part_recv_sem, d).wait_send()


def ceil_to(value, unit):
    return -(-value // unit) * unit


def solution(mesh):
    n = mesh.shape["ep"]

    def shards(images, reference_image, kernels, kernel_index, tile_mask, systematics, onsets):
        local, rows, width = images.shape
        side = kernels.shape[1]
        tiles = width // LANES
        block = rows // n
        epochs = local * n
        columns = systematics.shape[1] + onsets.shape[0]
        pack = max(LANES // epochs, 1)
        share = epochs // pack
        part_lanes = max(LANES, epochs)
        vmem = pl.BlockSpec(memory_space=pltpu.VMEM)
        smem = pl.BlockSpec(memory_space=pltpu.SMEM)
        dma = pltpu.SemaphoreType.DMA((n,))
        f32 = jnp.float32
        coefficients, epoch_scatter = pl.pallas_call(
            functools.partial(kernel, n),
            out_shape=(
                jax.ShapeDtypeStruct((columns, block * width), f32),
                jax.ShapeDtypeStruct((1, epochs), f32),
            ),
            in_specs=[vmem, vmem, vmem, smem, vmem, vmem, smem],
            out_specs=(vmem, vmem),
            scratch_shapes=[
                pltpu.VMEM((LANES, LANES), f32),
                pltpu.VMEM((LANES, LANES), f32),
                pltpu.VMEM((rows, ceil_to(side * rows, LANES)), f32),
                pltpu.VMEM((ceil_to(side * rows, LANES), width), f32),
                pltpu.VMEM((n, block * tiles * local, LANES), f32),
                pltpu.VMEM((n, block * tiles * local, LANES), f32),
                pltpu.VMEM((epochs, block * width), f32),
                pltpu.VMEM((share, part_lanes), f32),
                pltpu.VMEM((n, share, part_lanes), f32),
                pltpu.VMEM((epochs, ceil_to(2 * epochs + columns, LANES)), f32),
                dma,
                dma,
                dma,
                dma,
            ],
            compiler_params=pltpu.CompilerParams(collective_id=0, has_side_effects=True),
        )(
            images,
            reference_image,
            jnp.transpose(kernels, (1, 0, 2)),
            kernel_index,
            jnp.transpose(tile_mask, (0, 2, 1)),
            systematics,
            onsets,
        )
        return coefficients.reshape(columns, block, width), epoch_scatter.reshape(epochs)

    in_specs = (
        P(("field", "ep"), None, None),
        P("field", None),
        P(),
        P(("field", "ep")),
        P(("field", "ep"), None, None),
        P("field", None),
        P("field"),
    )
    out_specs = (P(None, ("field", "ep"), None), P("field"))
    return jax.shard_map(shards, mesh=mesh, in_specs=in_specs, out_specs=out_specs, check_vma=False)
```

time: 187 us -> 23.3 us (0.12)
  matrix products: 84.9 us -> 0 us
  blocking collectives: 57.7 us -> 0 us
  Pallas kernels: 0 us -> 19.9 us
  other arithmetic: 17.5 us -> 0 us
  local copies, waits for them, and re-layouts: 12 us -> 2.59 us
  starting transfers between devices: 7.41 us -> 0 us
  waiting for transfers between devices: 6.57 us -> 0 us
    conv_general_dilated x1 -> x0, matrix products: 82.8 us -> none  [one_strip(): lax.conv_general_dilated(piece[None], filters, (1, 1), 'VALID', dimension...]
    psum x1 -> x0, blocking collectives: 57.7 us -> none  [shards(): scatter = lax.psum(partial_value, 'ep')]
    pallas_call x0 -> x1, Pallas kernels: none -> 19.9 us  [shards(): pl.pallas_call(functools.partial(kernel, n), out_shape=(jax.ShapeDtypeStr...]
    another operation x10 -> x0, other arithmetic: 16.1 us -> none  [the longest x3 5.05 us: fit_matrix(): lower_fit = jnp.linalg.cholesky(normal)]
    broadcast_in_dim x3 -> x0, local copies, waits for them, and re-layouts: 8.86 us -> none  [the longest x2 8.6 us: one_strip(): piece[None]]
    all_to_all x1 -> x0, starting transfers between devices: 7.41 us -> none  [shards(): lax.all_to_all(difference, 'ep', split_axis=1, concat_axis=0, tiled=True)]
    all_to_all x1 -> x0, waiting for transfers between devices: 6.57 us -> none  [shards(): lax.all_to_all(difference, 'ep', split_axis=1, concat_axis=0, tiled=True)]
  transfers between devices with their start and end apart: 1 -> 0, of which waited for: 1 -> 0; matrix products, arithmetic and copies ran while one was open for 0% -> 0% of each run, Pallas kernels for 0% -> 0%
where the time goes in v1:
time: 23.3 us; the launch traced here: 23.1 us
  Pallas kernels  19.9 us (85%)
  local copies, waits for them, and re-layouts  2.59 us (11%)
  between operations  0.64 us (3%)
    pallas_call x1, Pallas kernels, shards(): pl.pallas_call(functools.partial(kernel, n), out_shape=(jax.ShapeDtypeStr...  19.9 us
    unnamed x4, local copies, waits for them, and re-layouts  2.59 us

profile of v1, /device:TPU:0, one launch (start us, length us, event | category | flops | bytes accessed | tf_op | source)
XLA Modules:
  0.0 23.1 jit_solution(11280127971570827914)
XLA Ops:
  0.6 19.9 %shard_map.86 = (f32[48,256]{1,0:T(8,128)}, f32[1,32]{1,0:T(1,128)}) custom-call(f32[2,16,256]{2,1,0:T(8,128)} %images_ref.1, f32[16,256]{1,0:T(8,128)} %reference_ref.1, f32[23,16,23]{2,1,0:T(8,128)} %bitcast.4, s32[2]{0:T(128)} %index_ref.1, s32[2,2,16]{2,1,0:T(2,128)} %bitcast.6, f32[32,40]{1,0:T(8,128)} %systematics_ref.1, s32[8]{0:T(128)} %onsets_ref.1), custom_call_target="tpu_custom_call" | custom-call | tf_op jit(solution)/shard_map/pallas_call | solution.py:224
  20.5 1.5 %copy.9 = f32[48,1,256]{2,1,0:T(1,128)} copy(f32[48,1,256]{2,0,1:T(8,128)} %bitcast.5) | data formatting | bytes 98304
  22.0 0.0 copy-start
  22.0 0.6 %copy-done = f32[1,32]{1,0:T(1,128)S(1)} copy-done((f32[1,32]{1,0:T(1,128)S(1)}, f32[1,32]{1,0:T(1,128)}, u32[]{:S(2)}) %copy-start) | copy-done | bytes 152
  22.6 0.5 %copy.11 = f32[32]{0:T(128)} copy(f32[32]{0:T(128)S(1)} %bitcast.7) | data formatting | bytes 256
Async XLA Ops:
  22.0 0.6 %copy-start = (f32[1,32]{1,0:T(1,128)S(1)}, f32[1,32]{1,0:T(1,128)}, u32[]{:S(2)}) copy-start(f32[1,32]{1,0:T(1,128)} %get-tuple-element.5) | copy-start | bytes 388

commit v2 on v1

--- a/solution.py
+++ b/solution.py
@@ -10,6 +10,7 @@
 cov_ridge = 0.5
 fit_ridge = 1.0
 LANES = 128
+VMEM_GRANT = 24 * 2**20
 HIGHEST = lax.Precision.HIGHEST
 
 
@@ -23,8 +24,18 @@
     return lax.broadcasted_iota(jnp.int32, shape, axis)
 
 
-def kernel(
+def exchange_kernel(
     n,
+    images_hbm,
+    reference_hbm,
+    kernels_hbm,
+    index_hbm,
+    mask_hbm,
+    systematics_hbm,
+    onsets_hbm,
+    pixels,
+    total_ref,
+    work,
     images_ref,
     reference_ref,
     kernels_ref,
@@ -32,18 +43,15 @@
     mask_ref,
     systematics_ref,
     onsets_ref,
-    coefficients_ref,
-    epoch_ref,
     table,
     table_t,
     taps,
     shifted,
     send,
     recv,
-    pixels,
     part,
     parts,
-    work,
+    load_sem,
     send_sem,
     recv_sem,
     part_send_sem,
@@ -58,7 +66,6 @@
     nsys = systematics_ref.shape[1]
     ntr = onsets_ref.shape[0]
     columns = nsys + ntr
-    npixels = float(rows * width)
     pack = max(LANES // epochs, 1)
     me = lax.axis_index("ep")
 
@@ -70,6 +77,25 @@
             device_id={"ep": lax.rem(me + d, n)},
             device_id_type=pl.DeviceIdType.MESH,
         )
+
+    loads = [
+        pltpu.make_async_copy(source, target, load_sem.at[i])
+        for i, (source, target) in enumerate(
+            (
+                (index_hbm, index_ref),
+                (kernels_hbm, kernels_ref),
+                (images_hbm, images_ref),
+                (mask_hbm, mask_ref),
+                (reference_hbm, reference_ref),
+                (systematics_hbm, systematics_ref),
+                (onsets_hbm, onsets_ref),
+            )
+        )
+    ]
+    for load in loads:
+        load.start()
+    for load in loads:
+        load.wait()
 
     depth = side * rows
     padded_depth = taps.shape[1]
@@ -138,6 +164,8 @@
     work[:, epochs + nsys : epochs + columns] = transient[:, 0:ntr]
     design = work[...]
     outer = dot(design, design, ((1,), (1,)))
+    diagonal = iota((epochs, epochs), 0) == iota((epochs, epochs), 1)
+    ridge = jnp.where(diagonal, cov_ridge, 0.0)
 
     for d in range(1, n):
         source = lax.rem(me - d + n, n)
@@ -152,8 +180,9 @@
     partial_scatter = dot(data, data, ((1,), (1,)))
     share = epochs // pack
     if pack > 1:
-        work[:, 0:epochs] = partial_scatter
-        wide = jnp.where(iota((epochs, work.shape[1]), 1) < epochs, work[...], 0.0)[:, 0:LANES]
+        table[0:epochs, :] = jnp.zeros((epochs, LANES), jnp.float32)
+        table[0:epochs, 0:epochs] = partial_scatter
+        wide = table[0:epochs, :]
         packed = wide[0:share, :]
         for j in range(1, pack):
             packed = packed + pltpu.roll(wide[j * share : (j + 1) * share, :], j * epochs, axis=1)
@@ -169,6 +198,20 @@
     total = parts[0]
     for j in range(1, n):
         total = total + parts[j]
+    total_ref[...] = total
+    work[:, 0:epochs] = fit_ridge * outer + ridge
+    work[:, epochs + columns : 2 * epochs + columns] = ridge
+
+    for d in range(1, n):
+        exchange(send.at[lax.rem(me + d, n)], recv.at[me], send_sem, recv_sem, d).wait_send()
+        exchange(part, parts.at[me], part_send_sem, part_recv_sem, d).wait_send()
+
+
+def fit_kernel(npixels, pixels_ref, total_ref, base_ref, coefficients_ref, epoch_ref, work):
+    columns, block, width = coefficients_ref.shape
+    epochs = pixels_ref.shape[0]
+    pack = epochs // total_ref.shape[0]
+    total = total_ref[...]
     if pack > 1:
         pieces = [total] + [
             pltpu.roll(total, LANES - j * epochs, axis=1) for j in range(1, pack)
@@ -177,11 +220,11 @@
     else:
         scatter = total
 
-    diagonal = iota((epochs, epochs), 0) == iota((epochs, epochs), 1)
-    covariance = scatter * (1.0 / npixels) + jnp.where(diagonal, cov_ridge, 0.0)
-    work[:, 0:epochs] = covariance + fit_ridge * outer
+    covariance = scatter * (1.0 / npixels)
+    work[...] = jnp.zeros_like(work)
+    work[:, 0:epochs] = covariance
     work[:, epochs + columns : 2 * epochs + columns] = covariance
-    system = work[...]
+    system = work[...] + base_ref[...]
     index = iota(system.shape, 0)
     for k in range(epochs):
         pivot_row = system[k : k + 1, :]
@@ -189,15 +232,12 @@
         scaled = pivot_row * (1.0 / system[k : k + 1, k : k + 1])
         system = jnp.where(index == k, scaled, system - factor * scaled)
 
-    fitted = dot(system, data, ((0,), (0,)))
-    coefficients_ref[...] = fitted[epochs : epochs + columns, :]
+    fitted = dot(system, pixels_ref[...], ((0,), (0,)))[epochs : epochs + columns, :]
+    for q in range(block):
+        coefficients_ref[:, q, :] = fitted[:, q * width : (q + 1) * width]
     product = dot(scatter, system, ((1,), (0,))) * system
     work[0:1, :] = jnp.sum(product, axis=0, keepdims=True) * (1.0 / npixels)
-    epoch_ref[...] = work[0:1, epochs + columns : 2 * epochs + columns]
-
-    for d in range(1, n):
-        exchange(send.at[lax.rem(me + d, n)], recv.at[me], send_sem, recv_sem, d).wait_send()
-        exchange(part, parts.at[me], part_send_sem, part_recv_sem, d).wait_send()
+    epoch_ref[...] = work[0, epochs + columns : 2 * epochs + columns]
 
 
 def ceil_to(value, unit):
@@ -218,44 +258,70 @@
         share = epochs // pack
         part_lanes = max(LANES, epochs)
         vmem = pl.BlockSpec(memory_space=pltpu.VMEM)
-        smem = pl.BlockSpec(memory_space=pltpu.SMEM)
         dma = pltpu.SemaphoreType.DMA((n,))
         f32 = jnp.float32
-        coefficients, epoch_scatter = pl.pallas_call(
-            functools.partial(kernel, n),
+        flat_kernels = jnp.transpose(kernels, (1, 0, 2))
+        flat_mask = jnp.transpose(tile_mask, (0, 2, 1))
+        system_lanes = ceil_to(2 * epochs + columns, LANES)
+        pixels, total, base = pl.pallas_call(
+            functools.partial(exchange_kernel, n),
             out_shape=(
-                jax.ShapeDtypeStruct((columns, block * width), f32),
-                jax.ShapeDtypeStruct((1, epochs), f32),
+                jax.ShapeDtypeStruct((epochs, block * width), f32),
+                jax.ShapeDtypeStruct((share, part_lanes), f32),
+                jax.ShapeDtypeStruct((epochs, system_lanes), f32),
             ),
-            in_specs=[vmem, vmem, vmem, smem, vmem, vmem, smem],
-            out_specs=(vmem, vmem),
+            in_specs=[pl.BlockSpec(memory_space=pltpu.HBM)] * 7,
+            out_specs=(vmem, vmem, vmem),
             scratch_shapes=[
+                pltpu.VMEM(images.shape, f32),
+                pltpu.VMEM(reference_image.shape, f32),
+                pltpu.VMEM(flat_kernels.shape, f32),
+                pltpu.SMEM(kernel_index.shape, jnp.int32),
+                pltpu.VMEM(flat_mask.shape, jnp.int32),
+                pltpu.VMEM(systematics.shape, f32),
+                pltpu.SMEM(onsets.shape, jnp.int32),
                 pltpu.VMEM((LANES, LANES), f32),
                 pltpu.VMEM((LANES, LANES), f32),
                 pltpu.VMEM((rows, ceil_to(side * rows, LANES)), f32),
                 pltpu.VMEM((ceil_to(side * rows, LANES), width), f32),
                 pltpu.VMEM((n, block * tiles * local, LANES), f32),
                 pltpu.VMEM((n, block * tiles * local, LANES), f32),
-                pltpu.VMEM((epochs, block * width), f32),
                 pltpu.VMEM((share, part_lanes), f32),
                 pltpu.VMEM((n, share, part_lanes), f32),
-                pltpu.VMEM((epochs, ceil_to(2 * epochs + columns, LANES)), f32),
+                pltpu.SemaphoreType.DMA((7,)),
                 dma,
                 dma,
                 dma,
                 dma,
             ],
-            compiler_params=pltpu.CompilerParams(collective_id=0, has_side_effects=True),
+            compiler_params=pltpu.CompilerParams(
+                collective_id=0, has_side_effects=True, vmem_limit_bytes=VMEM_GRANT
+            ),
         )(
-            images,
-            reference_image,
-            jnp.transpose(kernels, (1, 0, 2)),
-            kernel_index,
-            jnp.transpose(tile_mask, (0, 2, 1)),
-            systematics,
-            onsets,
+            *(
+                pltpu.with_memory_space_constraint(value, pltpu.HBM)
+                for value in (
+                    images,
+                    reference_image,
+                    flat_kernels,
+                    kernel_index,
+                    flat_mask,
+                    systematics,
+                    onsets,
+                )
+            )
         )
-        return coefficients.reshape(columns, block, width), epoch_scatter.reshape(epochs)
+        return pl.pallas_call(
+            functools.partial(fit_kernel, float(rows * width)),
+            out_shape=(
+                jax.ShapeDtypeStruct((columns, block, width), f32),
+                jax.ShapeDtypeStruct((epochs,), f32),
+            ),
+            in_specs=[vmem, vmem, vmem],
+            out_specs=(vmem, vmem),
+            scratch_shapes=[pltpu.VMEM((epochs, system_lanes), f32)],
+            compiler_params=pltpu.CompilerParams(vmem_limit_bytes=VMEM_GRANT),
+        )(pixels, total, base)
 
     in_specs = (
         P(("field", "ep"), None, None),

time: 23.3 us -> 19.8 us (0.85)
  local copies, waits for them, and re-layouts: 2.59 us -> 0 us
  Pallas kernels: 19.9 us -> 19 us
    unnamed x4 -> x0, local copies, waits for them, and re-layouts: 2.59 us -> none
    pallas_call x1 -> x2, Pallas kernels: 19.9 us -> 19 us  [the longest x1 15.3 us: shards(): pl.pallas_call(functools.partial(exchange_kernel, n), out_shape=(jax.Shap...]
where the time goes in v2:
time: 19.8 us; the launch traced here: 19.7 us
  Pallas kernels  19 us (96%)
  between operations  0.64 us (3%)
    pallas_call x1, Pallas kernels, shards(): pl.pallas_call(functools.partial(exchange_kernel, n), out_shape=(jax.Shap...  15.3 us
    pallas_call x1, Pallas kernels, shards(): pl.pallas_call(functools.partial(fit_kernel, float(rows * width)), out_sh...  3.71 us

profile of v2, /device:TPU:0, one launch (start us, length us, event | category | flops | bytes accessed | tf_op | source)
XLA Modules:
  0.0 19.7 jit_solution(5166712594394117516)
XLA Ops:
  0.6 15.3 %shard_map.86 = (f32[32,256]{1,0:T(8,128)S(1)}, f32[8,128]{1,0:T(8,128)S(1)}, f32[32,128]{1,0:T(8,128)S(1)}) custom-call(f32[2,16,256]{2,1,0:T(8,128)} %images_hbm.1, f32[16,256]{1,0:T(8,128)} %reference_hbm.1, f32[23,16,23]{2,1,0:T(8,128)} %bitcast.2, s32[2]{0:T(128)} %index_hbm.1, s32[2,2,16]{2,1,0:T(2,128)} %bitcast.3, f32[32,40]{1,0:T(8,128)} %systematics_hbm.1, ...), custom_call_target="tpu_custom_call" | custom-call | tf_op jit(solution)/shard_map/pallas_call | solution.py:266
  15.9 3.7 %shard_map.87 = (f32[48,1,256]{2,1,0:T(1,128)}, f32[32]{0:T(128)}) custom-call(f32[32,256]{1,0:T(8,128)S(1)} %get-tuple-element.5.pixels_ref, f32[8,128]{1,0:T(8,128)S(1)} %get-tuple-element.6.total_ref, f32[32,128]{1,0:T(8,128)S(1)} %get-tuple-element.7.base_ref), custom_call_target="tpu_custom_call" | custom-call | tf_op jit(solution)/shard_map/pallas_call | solution.py:314

commit v3 on v2

--- a/solution.py
+++ b/solution.py
@@ -225,12 +225,32 @@
     work[:, 0:epochs] = covariance
     work[:, epochs + columns : 2 * epochs + columns] = covariance
     system = work[...] + base_ref[...]
-    index = iota(system.shape, 0)
-    for k in range(epochs):
-        pivot_row = system[k : k + 1, :]
-        factor = system[:, k : k + 1]
-        scaled = pivot_row * (1.0 / system[k : k + 1, k : k + 1])
-        system = jnp.where(index == k, scaled, system - factor * scaled)
+    lanes = system.shape[1]
+    group = (8, lanes)
+    strips = [system[i : i + 8, :] for i in range(0, epochs, 8)]
+    index = iota(group, 0)
+
+    def spread(value, row):
+        return jnp.broadcast_to(value[row : row + 1, :], group)
+
+    for home in range(epochs // 8):
+        spans = [
+            [jnp.broadcast_to(strip[:, k : k + 1], group) for strip in strips]
+            for k in range(home * 8, home * 8 + 8)
+        ]
+        for row in range(8):
+            factors = spans[row]
+            inverse = 1.0 / spread(factors[home], row)
+
+            def step(values):
+                scaled = spread(values[home], row) * inverse
+                values = [v - f * scaled for v, f in zip(values, factors)]
+                values[home] = jnp.where(index == row, scaled, values[home])
+                return values
+
+            spans = [step(span) if j > row else span for j, span in enumerate(spans)]
+            strips = step(strips)
+    system = jnp.concatenate(strips, axis=0)
 
     fitted = dot(system, pixels_ref[...], ((0,), (0,)))[epochs : epochs + columns, :]
     for q in range(block):

time: 19.8 us -> 18.1 us (0.914)
  Pallas kernels: 19 us -> 17.3 us
    pallas_call x1, Pallas kernels: 3.71 us -> 2.02 us  [shards(): pl.pallas_call(functools.partial(fit_kernel, float(rows * width)), out_sh...]
where the time goes in v3:
time: 18.1 us; the launch traced here: 18 us
  Pallas kernels  17.3 us (96%)
  between operations  0.64 us (4%)
    pallas_call x1, Pallas kernels, shards(): pl.pallas_call(functools.partial(exchange_kernel, n), out_shape=(jax.Shap...  15.3 us
    pallas_call x1, Pallas kernels, shards(): pl.pallas_call(functools.partial(fit_kernel, float(rows * width)), out_sh...  2.02 us

profile of v3, /device:TPU:0, one launch (start us, length us, event | category | flops | bytes accessed | tf_op | source)
XLA Modules:
  0.0 18.0 jit_solution(16170451809852819868)
XLA Ops:
  0.6 15.3 %shard_map.86 = (f32[32,256]{1,0:T(8,128)S(1)}, f32[8,128]{1,0:T(8,128)S(1)}, f32[32,128]{1,0:T(8,128)S(1)}) custom-call(f32[2,16,256]{2,1,0:T(8,128)} %images_hbm.1, f32[16,256]{1,0:T(8,128)} %reference_hbm.1, f32[23,16,23]{2,1,0:T(8,128)} %bitcast.2, s32[2]{0:T(128)} %index_hbm.1, s32[2,2,16]{2,1,0:T(2,128)} %bitcast.3, f32[32,40]{1,0:T(8,128)} %systematics_hbm.1, ...), custom_call_target="tpu_custom_call" | custom-call | tf_op jit(solution)/shard_map/pallas_call | solution.py:286
  15.9 2.0 %shard_map.87 = (f32[48,1,256]{2,1,0:T(1,128)}, f32[32]{0:T(128)}) custom-call(f32[32,256]{1,0:T(8,128)S(1)} %get-tuple-element.5.pixels_ref, f32[8,128]{1,0:T(8,128)S(1)} %get-tuple-element.6.total_ref, f32[32,128]{1,0:T(8,128)S(1)} %get-tuple-element.7.base_ref), custom_call_target="tpu_custom_call" | custom-call | tf_op jit(solution)/shard_map/pallas_call | solution.py:334

commit v4 on v3

--- a/solution.py
+++ b/solution.py
@@ -147,7 +147,7 @@
             device_id_type=pl.DeviceIdType.MESH,
         )
 
-    for d in range(1, n):
+    for d in (*range(2, n, 2), *range(1, n, 2)):
         exchange(send.at[lax.rem(me + d, n)], recv.at[me], send_sem, recv_sem, d).start()
     recv[me] = send[me]
 
@@ -189,7 +189,7 @@
         part[...] = packed
     else:
         part[...] = partial_scatter
-    for d in range(1, n):
+    for d in (*range(2, n, 2), *range(1, n, 2)):
         exchange(part, parts.at[me], part_send_sem, part_recv_sem, d).start()
     parts[me] = part[...]
     for d in range(1, n):
@@ -238,17 +238,26 @@
             [jnp.broadcast_to(strip[:, k : k + 1], group) for strip in strips]
             for k in range(home * 8, home * 8 + 8)
         ]
-        for row in range(8):
-            factors = spans[row]
-            inverse = 1.0 / spread(factors[home], row)
+        for row in range(0, 8, 2):
+            lefts, rights = spans[row], spans[row + 1]
+            a, b = spread(lefts[home], row), spread(rights[home], row)
+            c, d = spread(lefts[home], row + 1), spread(rights[home], row + 1)
+            inverse = 1.0 / (a * d - b * c)
 
             def step(values):
-                scaled = spread(values[home], row) * inverse
-                values = [v - f * scaled for v, f in zip(values, factors)]
-                values[home] = jnp.where(index == row, scaled, values[home])
+                first, second = spread(values[home], row), spread(values[home], row + 1)
+                upper = (d * first - b * second) * inverse
+                lower = (a * second - c * first) * inverse
+                values = [
+                    v - left * upper - right * lower
+                    for v, left, right in zip(values, lefts, rights)
+                ]
+                values[home] = jnp.where(
+                    index == row, upper, jnp.where(index == row + 1, lower, values[home])
+                )
                 return values
 
-            spans = [step(span) if j > row else span for j, span in enumerate(spans)]
+            spans = [step(span) if j > row + 1 else span for j, span in enumerate(spans)]
             strips = step(strips)
     system = jnp.concatenate(strips, axis=0)
 

time: 18.1 us -> 17.9 us (0.989)
  Pallas kernels: 17.3 us -> 17.1 us
where the time goes in v4:
time: 17.9 us; the launch traced here: 17.7 us
  Pallas kernels  17.1 us (96%)
  between operations  0.64 us (4%)
    pallas_call x1, Pallas kernels, shards(): pl.pallas_call(functools.partial(exchange_kernel, n), out_shape=(jax.Shap...  15.2 us
    pallas_call x1, Pallas kernels, shards(): pl.pallas_call(functools.partial(fit_kernel, float(rows * width)), out_sh...  1.87 us

profile of v4, /device:TPU:0, one launch (start us, length us, event | category | flops | bytes accessed | tf_op | source)
XLA Modules:
  0.0 17.7 jit_solution(6895730538752509322)
XLA Ops:
  0.6 15.2 %shard_map.86 = (f32[32,256]{1,0:T(8,128)S(1)}, f32[8,128]{1,0:T(8,128)S(1)}, f32[32,128]{1,0:T(8,128)S(1)}) custom-call(f32[2,16,256]{2,1,0:T(8,128)} %images_hbm.1, f32[16,256]{1,0:T(8,128)} %reference_hbm.1, f32[23,16,23]{2,1,0:T(8,128)} %bitcast.2, s32[2]{0:T(128)} %index_hbm.1, s32[2,2,16]{2,1,0:T(2,128)} %bitcast.3, f32[32,40]{1,0:T(8,128)} %systematics_hbm.1, ...), custom_call_target="tpu_custom_call" | custom-call | tf_op jit(solution)/shard_map/pallas_call | solution.py:295
  15.8 1.9 %shard_map.87 = (f32[48,1,256]{2,1,0:T(1,128)}, f32[32]{0:T(128)}) custom-call(f32[32,256]{1,0:T(8,128)S(1)} %get-tuple-element.5.pixels_ref, f32[8,128]{1,0:T(8,128)S(1)} %get-tuple-element.6.total_ref, f32[32,128]{1,0:T(8,128)S(1)} %get-tuple-element.7.base_ref), custom_call_target="tpu_custom_call" | custom-call | tf_op jit(solution)/shard_map/pallas_call | solution.py:343
